TPU v7x, 128 devices: a whole 4x4x4 slice. The times are simulated.
128 devices in a mesh: row: 8 (over z, core), col: 16 (over x, y).
Axes of the slice: x: 4, y: 4, z: 4, core: 2. Of those that a mesh axis runs over, the one named last changes fastest.
Arguments:
- trial_factor: bfloat16 [2, 8192, 512], P(None, ('row', 'col')), may hold values from -6 to 6
- occupied: bfloat16 [8192, 512], P(('col', 'row')), may hold values from -0.25 to 0.25
- centers: float32 [3, 8192], P(None, ('row', 'col')), may hold values from 0 to 1
- exponents: float32 [8192], P(('row', 'col')), may hold values from 0.5 to 4
- wave_vectors: float32 [3, 8192], P(None, ('row', 'col')), may hold values from -36 to 36
- phases: float32 [8192], P(('row', 'col')), may hold values from -3.140625 to 3.140625
- points: float32 [256, 3, 1024], P(('row', 'col')), may hold values from 0 to 1
- density: float32 [256, 1024], P(('row', 'col')), may hold values from 0.05 to 1
- weights: float32 [256, 1024], P(('row', 'col')), may hold values from 0.0001 to 0.001
- sources: int32 [256, 8, 1], P(('row', 'col')), may hold values from 0 to 15; in each aligned block of 16 rows (0 to 15, 16 to 31, ..., all dimensions but the last counted through in order) at most 2 rows name the same one
Outputs:
- response: float32 [8192, 2, 512], P(('row', 'col'))
Inputs may be any that keep to these rules, and one draw needn't show every extreme that they name: `sources`: among the 16 entries of the batches of one device, no column block is named more than 2 times, and some block exactly 2 times.
All inputs are finite; a program needn't handle non-finite values.
Results may differ from a plain program's by a relative error of at most 0.0065.
Values may be sent and summed in bfloat16 or wider, within the bound.
A program may use at most 128 MiB of HBM per device.

v0:
```python
import jax
import jax.numpy as jnp
from jax import lax
from jax.sharding import PartitionSpec as P

TB = 256
EXCHANGE_COEF = 0.75 * (3.0 / 3.141592653589793) ** (1.0 / 3.0)


def rows_first(arrays, axis, dims):
    turned = [jnp.moveaxis(a, dim, 0) for a, dim in zip(arrays, dims)]
    both = jnp.concatenate([t.reshape(len(t), -1) for t in turned], axis=1)
    filled, at, finished = (lax.all_gather(both, axis, axis=0, tiled=True), 0, [])
    for t, dim in zip(turned, dims):
        slab = filled[:, at : at + t[0].size].reshape(-1, *t.shape[1:])
        finished.append(jnp.moveaxis(slab, 0, dim))
        at += t[0].size
    return tuple(finished)


def joined_along(tiles, dim):
    tiles = jnp.moveaxis(tiles, 0, dim)
    shape = tiles.shape
    return tiles.reshape(*shape[:dim], shape[dim] * shape[dim + 1], *shape[dim + 2 :])


def sent_to_all(value, axis):
    size = lax.axis_size(axis)
    return lax.all_to_all(
        jnp.broadcast_to(value[None], (size, *value.shape)), axis, 0, 0, tiled=True
    )


def gather_directly(value, axis, dim):
    return joined_along(sent_to_all(value, axis), dim)


def split_up(value, dim, size):
    shape = value.shape
    tiles = value.reshape(*shape[:dim], size, shape[dim] // size, *shape[dim + 1 :])
    return jnp.moveaxis(tiles, dim, 0)


def sum_at_owner(value, axis, dim):
    size = lax.axis_size(axis)
    tiles = lax.all_to_all(split_up(value, dim, size), axis, 0, 0, tiled=True)
    return jnp.sum(tiles.astype(jnp.float32), axis=0)


def collocate(grid_points, func_centers, func_exponents, func_waves, func_phases):
    npoints = grid_points.shape[1]
    nfuncs = func_centers.shape[1]
    radius = jnp.zeros((npoints, nfuncs), jnp.float32)
    phase_sum = jnp.zeros((npoints, nfuncs), jnp.float32) + func_phases[None, :]
    for coordinate in range(3):
        offset = grid_points[coordinate][:, None] - func_centers[coordinate][None, :]
        radius = radius + offset * offset
        phase_sum = phase_sum + grid_points[coordinate][:, None] * func_waves[coordinate][None, :]
    return (jnp.exp(-func_exponents[None, :] * radius) * jnp.cos(phase_sum)).astype(jnp.bfloat16)


def batch_response(ground, quad_weights, row_values, col_values, pair_tiles):
    npoints = col_values.shape[0]
    row_tiles = pair_tiles.shape[0]
    col_span = pair_tiles.shape[1]
    tile_width = pair_tiles.shape[2]
    tile_size = row_values.shape[1] // row_tiles
    vectors = tile_width // tile_size
    col_phi = col_values.reshape(npoints, row_tiles, col_span)
    half_contracted = jnp.einsum(
        "gax,axy->gay", col_phi, pair_tiles, preferred_element_type=jnp.float32
    )
    half_contracted = half_contracted.reshape(npoints, row_tiles, vectors, tile_size)
    row_phi = row_values.astype(jnp.float32).reshape(npoints, row_tiles, 1, tile_size)
    response_density = jnp.sum(half_contracted * row_phi, axis=(1, 3))
    kernel = -(4.0 / 9.0) * EXCHANGE_COEF * jnp.exp(-(2.0 / 3.0) * jnp.log(ground))
    potential = (quad_weights * kernel)[:, None] * response_density
    scaled = (
        (potential[:, None, :, None] * row_phi)
        .astype(jnp.bfloat16)
        .reshape(npoints, row_tiles, tile_width)
    )
    matrix = jnp.einsum("gax,gay->axy", col_phi, scaled, preferred_element_type=jnp.float32)
    return matrix.astype(jnp.bfloat16)


def per_device(
    trial_factor,
    occupied,
    centers,
    exponents,
    wave_vectors,
    phases,
    points,
    density,
    weights,
    sources,
):
    columns = lax.axis_size("col")
    row_block = lax.axis_index("row")
    all_centers, all_waves, all_exponents, all_phases = rows_first(
        (centers, wave_vectors, exponents, phases), ("row", "col"), (1, 1, 0, 0)
    )
    col_factor = gather_directly(occupied, "row", 0)
    span_col = col_factor.shape[0]
    orbital_count = col_factor.shape[1]
    tiles_col = span_col // TB
    span_row = trial_factor.shape[1] * columns
    tiles_row = span_row // TB
    vectors = trial_factor.shape[0]
    pair_count = tiles_row * tiles_col
    batch_count = sources.shape[0]
    slot_count = batch_count * pair_count
    slot_source = sources.reshape(slot_count)
    capacity = max(2, (slot_count + columns - 1) // columns)
    source_hot = (slot_source[:, None] == jnp.arange(columns, dtype=jnp.int32)[None, :]).astype(
        jnp.int32
    )
    slot_rank = jnp.sum(source_hot * (jnp.cumsum(source_hot, axis=0) - 1), axis=1)
    slot_place = slot_source * capacity + slot_rank
    slot_pair = jnp.arange(slot_count, dtype=jnp.int32) % pair_count
    place_hot = slot_place[:, None] == jnp.arange(columns * capacity, dtype=jnp.int32)[None, :]
    place_matrix = place_hot.astype(jnp.bfloat16)
    wanted = jnp.sum(place_hot.astype(jnp.int32) * (slot_pair[:, None] + 1), axis=0) - 1
    asked_pairs = lax.all_to_all(
        wanted.reshape(columns, capacity), "col", split_axis=0, concat_axis=0, tiled=True
    )
    asked_flat = asked_pairs.reshape(columns * capacity)
    asked_col = jnp.where(asked_flat >= 0, asked_flat % tiles_col, -1)
    col_hot = (asked_col[:, None] == jnp.arange(tiles_col, dtype=jnp.int32)[None, :]).astype(
        jnp.bfloat16
    )
    row_start = row_block * span_row
    row_centers = lax.dynamic_slice_in_dim(all_centers, row_start, span_row, 1)
    row_waves = lax.dynamic_slice_in_dim(all_waves, row_start, span_row, 1)
    row_exponents = lax.dynamic_slice_in_dim(all_exponents, row_start, span_row, 0)
    row_phases = lax.dynamic_slice_in_dim(all_phases, row_start, span_row, 0)
    tile_offsets = jnp.arange(TB, dtype=jnp.int32)
    column_tile = slot_source * tiles_col + slot_pair % tiles_col
    column_index = (column_tile[:, None] * TB + tile_offsets[None, :]).reshape(
        batch_count, pair_count * TB
    )
    row_trial = gather_directly(trial_factor, "col", 1)
    row_split = row_trial.reshape(vectors, tiles_row, TB, orbital_count)
    outgoing_rows = (
        jnp.dot(
            col_hot,
            col_factor.reshape(tiles_col, TB * orbital_count),
            preferred_element_type=jnp.float32,
        )
        .astype(jnp.bfloat16)
        .reshape(columns, capacity, TB * orbital_count)
    )
    incoming_rows = lax.all_to_all(outgoing_rows, "col", split_axis=0, concat_axis=0, tiled=True)
    slot_rows = jnp.dot(
        place_matrix,
        incoming_rows.reshape(columns * capacity, TB * orbital_count),
        preferred_element_type=jnp.float32,
    ).astype(jnp.bfloat16)
    slot_rows = slot_rows.reshape(batch_count, tiles_row, tiles_col * TB, orbital_count)
    accumulated = jnp.zeros((span_row, vectors, orbital_count), jnp.float32)
    for position in range(batch_count):
        factor_rows = slot_rows[position]
        tiles_now = (
            jnp.einsum("kami,axi->axkm", row_split, factor_rows, preferred_element_type=jnp.float32)
            .astype(jnp.bfloat16)
            .reshape(tiles_row, tiles_col * TB, vectors * TB)
        )
        index_now = column_index[position]
        row_values = collocate(points[position], row_centers, row_exponents, row_waves, row_phases)
        col_values = collocate(
            points[position],
            jnp.take(all_centers, index_now, axis=1),
            jnp.take(all_exponents, index_now),
            jnp.take(all_waves, index_now, axis=1),
            jnp.take(all_phases, index_now),
        )
        potential_now = batch_response(
            density[position], weights[position], row_values, col_values, tiles_now
        )
        contrib = jnp.einsum(
            "axkm,axi->amki",
            potential_now.reshape(tiles_row, tiles_col * TB, vectors, TB),
            factor_rows,
            preferred_element_type=jnp.float32,
        )
        accumulated = accumulated + contrib.reshape(span_row, vectors, orbital_count)
    return sum_at_owner(accumulated.astype(jnp.bfloat16), "col", 0)


def solution(mesh):
    in_specs = (
        P(None, ("row", "col"), None),
        P(("col", "row"), None),
        P(None, ("row", "col")),
        P(("row", "col")),
        P(None, ("row", "col")),
        P(("row", "col")),
        P(("row", "col"), None, None),
        P(("row", "col"), None),
        P(("row", "col"), None),
        P(("row", "col"), None, None),
    )
    out_specs = P(("row", "col"), None, None)
    return jax.shard_map(
        per_device, mesh=mesh, in_specs=in_specs, out_specs=out_specs, check_vma=False
    )
```

profile of v0, /device:TPU:0, one launch (start us, length us, event | category | flops | bytes accessed | tf_op | source)
XLA Modules:
  0.0 501.2 jit_solution(6194793369204841043)
XLA Ops:
  2.4 14.6 %all_to_all.26 = s32[16,1,2]{2,1,0:T(1,128)S(1)} all-to-all(s32[16,1,2]{2,1,0:T(1,128)S(1)} %bitcast.131), channel_id=1, replica_groups=mesh['row'=8,'col'=16] {'col'}, dimensions={0} | all-to-all | bytes 256 | tf_op jit(solution)/shard_map/all_to_all | solution.py:125
  17.9 15.5 %all_to_all.27 = bf16[8,64,512]{2,1,0:T(8,128)(2,1)S(1)} all-to-all(bf16[8,64,512]{2,1,0:T(8,128)(2,1)S(1)} %broadcast_in_dim.16), channel_id=1, replica_groups=mesh['row'=8,'col'=16] {'row'}, dimensions={0} | all-to-all | bytes 1048576 | tf_op jit(solution)/shard_map/all_to_all | solution.py:29
  39.7 73.3 %all-gather = f32[128,64,8]{1,2,0:T(8,128)S(1)} all-gather(f32[1,64,8]{1,2,0:T(8,128)S(1)} %maximum_bitcast_fusion), channel_id=1, replica_groups=mesh['row'=8,'col'=16] {'row','col'}, dimensions={0}, use_global_device_ids=true | all-gather | bytes 264192 | tf_op jit(solution)/shard_map/all_gather | solution.py:13
  116.8 5.6 %convolution_convert_fusion = bf16[32,131072]{1,0:T(8,128)(2,1)} fusion(bf16[2,131072]{1,0:T(2,128)(2,1)S(1)} %reshape_reshape.6, s32[32]{0:T(128)S(1)} %compare_select_fusion.6), kind=kOutput, calls=%fused_computation.8 | convolution fusion | flops 20971584 | bytes 8913024 | tf_op jit(solution)/shard_map/dot_general | solution.py:146
  122.4 9.4 %reshape.626 = bf16[16,2,131072]{2,1,0:T(2,128)(2,1)} reshape(bf16[32,131072]{1,0:T(8,128)(2,1)} %convolution_convert_fusion) | data formatting | bytes 16777216 | tf_op jit(solution)/shard_map/reshape | solution.py:152
  133.1 5.3 %all-to-all-start.2 = ((bf16[16,2,131072]{2,1,0:T(2,128)(2,1)}), bf16[16,2,131072]{2,1,0:T(2,128)(2,1)}, u32[]{:S(2)}, u32[]{:S(2)}) async-start(bf16[16,2,131072]{2,1,0:T(2,128)(2,1)} %reshape.626), calls=%async_computation.2 | async-start | bytes 16777216 | tf_op jit(solution)/shard_map/all_to_all | solution.py:154
  138.4 9.0 %slice_reduce_fusion.19 = (f32[8192]{0:T(1024)S(1)}, f32[8192]{0:T(1024)S(1)}, f32[8192,1]{1,0:T(8,128)}, f32[8192,1]{1,0:T(8,128)}) fusion(f32[8192,8]{1,0:T(8,128)} %bitcast.98), kind=kLoop, calls=%fused_computation.112 | loop fusion | bytes 196608 | tf_op jit(solution)/shard_map/slice | solution.py:15
  147.3 11.8 %gather_fusion.4 = f32[2048]{0:T(1024)S(1)} fusion(f32[8192]{0:T(1024)S(1)} %get-tuple-element.6, s32[2048]{0:T(1024)S(1)} %fusion.27), kind=kCustom, calls=%fused_computation.3.clone | custom fusion | bytes 24576 | tf_op jit(solution)/shard_map/jit(_take)/gather | solution.py:174
  159.1 11.8 %gather_fusion = f32[2048]{0:T(1024)S(1)} fusion(f32[8192]{0:T(1024)S(1)} %get-tuple-element.6, s32[2048]{0:T(1024)S(1)} %fusion.26), kind=kCustom, calls=%fused_computation.clone | custom fusion | bytes 24576 | tf_op jit(solution)/shard_map/jit(_take)/gather | solution.py:174
  170.9 11.8 %gather_fusion.6 = f32[2048]{0:T(1024)S(1)} fusion(f32[8192]{0:T(1024)S(1)} %get-tuple-element.8, s32[2048]{0:T(1024)S(1)} %fusion.27), kind=kCustom, calls=%fused_computation.4.clone | custom fusion | bytes 24576 | tf_op jit(solution)/shard_map/jit(_take)/gather | solution.py:176
  182.7 11.8 %gather_fusion.2 = f32[2048]{0:T(1024)S(1)} fusion(f32[8192]{0:T(1024)S(1)} %get-tuple-element.8, s32[2048]{0:T(1024)S(1)} %fusion.26), kind=kCustom, calls=%fused_computation.2.clone | custom fusion | bytes 24576 | tf_op jit(solution)/shard_map/jit(_take)/gather | solution.py:176
  194.5 10.6 %slice_bitcast_fusion.3 = (f32[3,8192]{0,1:T(8,128)}, f32[3,8192]{0,1:T(8,128)}, f32[8192,3]{1,0:T(8,128)}, f32[8192,3]{1,0:T(8,128)}) fusion(f32[8192,8]{1,0:T(8,128)} %bitcast.99), kind=kLoop, calls=%fused_computation.111 | loop fusion | bytes 589824 | tf_op jit(solution)/shard_map/transpose | solution.py:16
  205.1 7.6 %gather_fusion.5 = f32[2048,3]{1,0:T(8,128)S(1)} fusion(f32[3,8192]{0,1:T(8,128)} %get-tuple-element.33, s32[2048]{0:T(1024)S(1)} %fusion.27), kind=kCustom, calls=%fused_computation.6.clone | custom fusion | bytes 57344 | tf_op jit(solution)/shard_map/jit(_take)/gather | solution.py:173
  212.7 7.6 %gather_fusion.1 = f32[2048,3]{1,0:T(8,128)S(1)} fusion(f32[3,8192]{0,1:T(8,128)} %get-tuple-element.33, s32[2048]{0:T(1024)S(1)} %fusion.26), kind=kCustom, calls=%fused_computation.1.clone | custom fusion | bytes 57344 | tf_op jit(solution)/shard_map/jit(_take)/gather | solution.py:173
  220.4 9.8 %gather_fusion.3 = f32[2048,3]{1,0:T(8,128)} fusion(f32[3,8192]{0,1:T(8,128)} %get-tuple-element.34, s32[2048]{0:T(1024)S(1)} %fusion.26), kind=kCustom, calls=%fused_computation.5.clone | custom fusion | bytes 57344 | tf_op jit(solution)/shard_map/jit(_take)/gather | solution.py:175
  230.1 9.9 %gather_fusion.7 = f32[2048,3]{1,0:T(8,128)} fusion(f32[3,8192]{0,1:T(8,128)} %get-tuple-element.34, s32[2048]{0:T(1024)S(1)} %fusion.27), kind=kCustom, calls=%fused_computation.7.clone | custom fusion | bytes 57344 | tf_op jit(solution)/shard_map/jit(_take)/gather | solution.py:175
  253.9 33.1 %fusion.5 = (f32[1024,4,256]{0,2,1:T(8,128)}, f32[1024,4,256]{0,2,1:T(8,128)}) fusion(f32[1024]{0:T(1024)S(1)} %bitcast.116, f32[1024]{0:T(1024)S(1)} %bitcast.119, f32[1024]{0:T(1024)S(1)} %bitcast.113, f32[4,256]{1,0:T(4,128)S(1)} %mul.505, f32[4,256]{1,0:T(4,128)S(1)} %mul.502, f32[4,256]{1,0:T(4,128)S(1)} %mul.499, f32[4,256]{1,0:T(4,128)S(1)} %add.256, ...), kind=kLoop, calls=%fused_computation.25 | loop fusion | flops 37748736 | bytes 8445952 | tf_op jit(solution)/shard_map/convert_element_type | solution.py:74
  288.6 8.6 %reshape.627 = bf16[32,131072]{1,0:T(8,128)(2,1)} reshape(bf16[16,2,131072]{2,1,0:T(2,128)(2,1)} %all-to-all-done.2) | data formatting | bytes 16777216 | tf_op jit(solution)/shard_map/reshape | solution.py:157
  297.2 4.7 convolution_convert_fusion.1
  313.6 33.8 %fusion.2 = f32[1024,512]{0,1:T(8,128)S(1)} fusion(f32[1024,4,256]{0,2,1:T(8,128)S(1)} %copy-done, bf16[4,512,512]{1,2,0:T(8,128)(2,1)S(1)} %bitcast.106, f32[4,512]{1,0:T(4,128)S(1)} %mul.529, f32[4,512]{1,0:T(4,128)S(1)} %mul.526, f32[4,512]{1,0:T(4,128)S(1)} %mul.523, f32[4,512]{1,0:T(4,128)S(1)} %add.263, f32[4,512]{1,0:T(4,128)S(1)} %sub.262, ...), kind=kOutput, calls=%fused_computation.16 | convolution fusion | flops 2186805248 | bytes 8466432 | tf_op jit(solution)/shard_map/gax,axy->gay/dot_general | solution.py:70
  347.6 33.6 %fusion = f32[1024,512]{0,1:T(8,128)S(1)} fusion(f32[1024,4,256]{0,2,1:T(8,128)S(1)} %copy-done.1, bf16[4,512,512]{1,2,0:T(8,128)(2,1)S(1)} %bitcast.105, f32[4,512]{1,0:T(4,128)S(1)} %mul.484, f32[4,512]{1,0:T(4,128)S(1)} %mul.481, f32[4,512]{1,0:T(4,128)S(1)} %mul.478, f32[4,512]{1,0:T(4,128)S(1)} %add.248, f32[4,512]{1,0:T(4,128)S(1)} %sub.235, ...), kind=kOutput, calls=%fused_computation.14 | convolution fusion | flops 2186805248 | bytes 8466432 | tf_op jit(solution)/shard_map/gax,axy->gay/dot_general | solution.py:70
  383.2 33.7 %convolution_convert_fusion.3 = bf16[4,512,512]{1,2,0:T(8,128)(2,1)S(1)} fusion(bf16[1024,4,512]{0,2,1:T(8,128)(2,1)S(1)} %fusion.1, f32[4,512]{1,0:T(4,128)S(1)} %mul.484, f32[4,512]{1,0:T(4,128)S(1)} %mul.481, f32[4,512]{1,0:T(4,128)S(1)} %mul.478, f32[4,512]{1,0:T(4,128)S(1)} %add.248, f32[4,512]{1,0:T(4,128)S(1)} %sub.235, f32[1024]{0:T(1024)S(1)} %bitcast.124, ...), kind=kOutput, calls=%fused_computation.38 | convolution fusion | flops 2184183808 | bytes 6369280 | tf_op jit(solution)/shard_map/gax,gay->axy/dot_general | solution.py:83
  420.0 42.9 %convolution_convert_fusion.2 = bf16[4,512,512]{1,2,0:T(8,128)(2,1)S(1)} fusion(bf16[1024,4,512]{0,2,1:T(8,128)(2,1)S(1)} %fusion.3, f32[4,512]{1,0:T(4,128)S(1)} %mul.529, f32[4,512]{1,0:T(4,128)S(1)} %mul.526, f32[4,512]{1,0:T(4,128)S(1)} %mul.523, f32[4,512]{1,0:T(4,128)S(1)} %add.263, f32[4,512]{1,0:T(4,128)S(1)} %sub.262, f32[1024]{0:T(1024)S(1)} %bitcast.118, ...), kind=kOutput, calls=%fused_computation.37 | convolution fusion | flops 2184183808 | bytes 6369280 | tf_op jit(solution)/shard_map/gax,gay->axy/dot_general | solution.py:83
  464.7 35.1 %all_to_all.28 = bf16[16,64,2,512]{3,1,2,0:T(8,128)(2,1)S(1)} all-to-all(bf16[16,64,2,512]{3,1,2,0:T(8,128)(2,1)S(1)} %copy.31), channel_id=1, replica_groups=mesh['row'=8,'col'=16] {'col'}, dimensions={0} | all-to-all | bytes 4194304 | tf_op jit(solution)/shard_map/all_to_all | solution.py:46
  (113 shorter events, 49.6 us)
Async XLA Ops:
  0.0 39.6 %copy-start.11 = (f32[64]{0:T(128)S(1)}, f32[64]{0:T(128)}, u32[]{:S(2)}) copy-start(f32[64]{0:T(128)} %param.19) | copy-start | bytes 772
  0.0 39.6 %copy-start.9 = (f32[3,64]{1,0:T(4,128)S(1)}, f32[3,64]{1,0:T(4,128)}, u32[]{:S(2)}) copy-start(f32[3,64]{1,0:T(4,128)} %param.18) | copy-start | bytes 2308
  0.0 39.6 %copy-start.12 = (f32[64]{0:T(128)S(1)}, f32[64]{0:T(128)}, u32[]{:S(2)}) copy-start(f32[64]{0:T(128)} %param.17) | copy-start | bytes 772
  0.0 39.7 %copy-start.10 = (f32[3,64]{1,0:T(4,128)S(1)}, f32[3,64]{1,0:T(4,128)}, u32[]{:S(2)}) copy-start(f32[3,64]{1,0:T(4,128)} %param.16) | copy-start | bytes 2308
  35.8 95.9 %all-to-all-start.3 = ((bf16[16,2,64,512]{3,2,1,0:T(8,128)(2,1)}), bf16[16,2,64,512]{3,2,1,0:T(8,128)(2,1)S(1)}, u32[]{:S(2)}, u32[]{:S(2)}) async-start(bf16[16,2,64,512]{3,2,1,0:T(8,128)(2,1)} %broadcast_in_dim.17), calls=%async_computation.3 | async-start | bytes 4194304 | tf_op jit(solution)/shard_map/all_to_all | solution.py:29
  131.7 1.4 copy-start.3
  133.1 155.5 %all-to-all-start.2 = ((bf16[16,2,131072]{2,1,0:T(2,128)(2,1)}), bf16[16,2,131072]{2,1,0:T(2,128)(2,1)}, u32[]{:S(2)}, u32[]{:S(2)}) async-start(bf16[16,2,131072]{2,1,0:T(2,128)(2,1)} %reshape.626), calls=%async_computation.2 | async-start | bytes 16777216 | tf_op jit(solution)/shard_map/all_to_all | solution.py:154
  249.2 4.5 copy-start.7
  249.2 4.5 copy-start.8
  249.3 4.6 copy-start.6
  253.8 33.1 %copy-start.4 = (bf16[16,2,64,512]{3,2,1,0:T(8,128)(2,1)S(1)}, bf16[16,2,64,512]{3,2,1,0:T(8,128)(2,1)}, u32[]{:S(2)}) copy-start(bf16[16,2,64,512]{3,2,1,0:T(8,128)(2,1)} %copy-done.3) | copy-start | bytes 6291460
  308.3 3.1 copy-start.2
  308.3 3.1 copy-start.5
  311.4 2.2 copy-start
  313.6 34.0 %copy-start.1 = (f32[1024,4,256]{0,2,1:T(8,128)S(1)}, f32[1024,4,256]{0,2,1:T(8,128)}, u32[]{:S(2)}) copy-start(f32[1024,4,256]{0,2,1:T(8,128)} %get-tuple-element.40) | copy-start | bytes 12582916
where the time goes:
time: 507 us; the launch traced here: 501 us
  matrix products  161 us (32%)
  local copies, waits for them, and re-layouts  148 us (29%)
  blocking collectives  138 us (27%)
  other arithmetic  44 us (9%)
  starting transfers between devices  8.98 us (2%)
    dot_general x2, matrix products, batch_response(): jnp.einsum('gax,gay->axy', col_phi, scaled, preferred_element_type=jnp.fl...  76.7 us
    all_gather x1, blocking collectives, rows_first(): lax.all_gather(both, axis, axis=0, tiled=True)  73.3 us
    dot_general x2, matrix products, batch_response(): jnp.einsum('gax,axy->gay', col_phi, pair_tiles, preferred_element_type=jn...  67.5 us
    all_to_all x1, blocking collectives, sum_at_owner(): tiles = lax.all_to_all(split_up(value, dim, size), axis, 0, 0, tiled=True)  35.1 us
    convert_element_type x1, other arithmetic, batch_response(): row_values.astype(jnp.float32).reshape(npoints, row_tiles, 1, tile_size)  33.1 us
    gather x2, local copies, waits for them, and re-layouts, per_device(): jnp.take(all_phases, index_now)  23.6 us
    gather x2, local copies, waits for them, and re-layouts, per_device(): jnp.take(all_exponents, index_now)  23.6 us
    gather x2, local copies, waits for them, and re-layouts, per_device(): jnp.take(all_waves, index_now, axis=1)  19.6 us
  transfers between devices with their start and end apart: 2, of which 0 were waited for; matrix products, arithmetic and copies ran while one was open for 34% of the time, Pallas kernels for 0%

commit v1 on v0

--- a/solution.py
+++ b/solution.py
@@ -10,7 +10,13 @@
 def rows_first(arrays, axis, dims):
     turned = [jnp.moveaxis(a, dim, 0) for a, dim in zip(arrays, dims)]
     both = jnp.concatenate([t.reshape(len(t), -1) for t in turned], axis=1)
-    filled, at, finished = (lax.all_gather(both, axis, axis=0, tiled=True), 0, [])
+    filled, at, finished = (
+        jnp.concatenate(
+            lax.all_to_all(jnp.stack([both for _ in range(lax.psum(1, axis))], 0), axis, 0, 0), 0
+        ),
+        0,
+        [],
+    )
     for t, dim in zip(turned, dims):
         slab = filled[:, at : at + t[0].size].reshape(-1, *t.shape[1:])
         finished.append(jnp.moveaxis(slab, 0, dim))

time: 507 us -> 463 us (0.913)
  blocking collectives: 138 us -> 62.9 us
  waiting for transfers between devices: 0.01 us -> 20.3 us
  starting transfers between devices: 8.98 us -> 16.1 us
    all_gather x1 -> x0, blocking collectives: 73.3 us -> none  [rows_first(): lax.all_gather(both, axis, axis=0, tiled=True)]
    all_to_all x1, waiting for transfers between devices: 0.01 us -> 13.9 us  [sent_to_all(): lax.all_to_all(jnp.broadcast_to(value[None], (size, *value.shape)), axis,...]
    all_to_all x0 -> x1, starting transfers between devices: none -> 7.15 us  [per_device(): lax.all_to_all(wanted.reshape(columns, capacity), 'col', split_axis=0, co...]
    all_to_all x0 -> x1, waiting for transfers between devices: none -> 6.4 us  [per_device(): lax.all_to_all(wanted.reshape(columns, capacity), 'col', split_axis=0, co...]
  transfers between devices with their start and end apart: 2 -> 3, of which waited for: 0 -> 2; matrix products, arithmetic and copies ran while one was open for 34% -> 38% of each run, Pallas kernels for 0% -> 0%
where the time goes in v1:
time: 463 us; the launch traced here: 457 us
  matrix products  161 us (35%)
  local copies, waits for them, and re-layouts  149 us (32%)
  blocking collectives  62.9 us (14%)
  other arithmetic  46.1 us (10%)
  waiting for transfers between devices  20.3 us (4%)
  starting transfers between devices  16.1 us (3%)
    dot_general x2, matrix products, batch_response(): jnp.einsum('gax,gay->axy', col_phi, scaled, preferred_element_type=jnp.fl...  76.7 us
    dot_general x2, matrix products, batch_response(): jnp.einsum('gax,axy->gay', col_phi, pair_tiles, preferred_element_type=jn...  67.5 us
    convert_element_type x1, other arithmetic, batch_response(): row_values.astype(jnp.float32).reshape(npoints, row_tiles, 1, tile_size)  33.1 us
    all_to_all x1, blocking collectives, sum_at_owner(): tiles = lax.all_to_all(split_up(value, dim, size), axis, 0, 0, tiled=True)  32.2 us
    gather x2, local copies, waits for them, and re-layouts, per_device(): jnp.take(all_phases, index_now)  23.6 us
    gather x2, local copies, waits for them, and re-layouts, per_device(): jnp.take(all_exponents, index_now)  23.6 us
    gather x2, local copies, waits for them, and re-layouts, per_device(): jnp.take(all_waves, index_now, axis=1)  19.6 us
    all_to_all x1, blocking collectives, rows_first(): lax.all_to_all(jnp.stack([both for _ in range(lax.psum(1, axis))], 0), ax...  17.9 us
  transfers between devices with their start and end apart: 3, of which 2 were waited for; matrix products, arithmetic and copies ran while one was open for 38% of the time, Pallas kernels for 0%

profile of v1, /device:TPU:0, one launch (start us, length us, event | category | flops | bytes accessed | tf_op | source)
XLA Modules:
  0.0 456.8 jit_solution(4045173567904288285)
XLA Ops:
  3.2 7.1 %all-to-all-start = ((s32[16,1,2]{2,1,0:T(1,128)}), s32[16,1,2]{2,1,0:T(1,128)S(1)}, u32[]{:S(2)}, u32[]{:S(2)}) async-start(s32[16,1,2]{2,1,0:T(1,128)} %bitcast), calls=%async_computation | async-start | bytes 16384 | tf_op jit(solution)/shard_map/all_to_all | solution.py:131
  11.4 6.4 %all-to-all-done = s32[16,1,2]{2,1,0:T(1,128)S(1)} async-done(((s32[16,1,2]{2,1,0:T(1,128)}), s32[16,1,2]{2,1,0:T(1,128)S(1)}, u32[]{:S(2)}, u32[]{:S(2)}) %all-to-all-start) | async-done | bytes 160 | tf_op jit(solution)/shard_map/all_to_all | solution.py:131
  17.8 17.9 %all_to_all.31 = f32[128,1,512]{2,1,0:T(1,128)S(1)} all-to-all(f32[128,1,512]{2,1,0:T(1,128)S(1)} %reshape.774), channel_id=1, replica_groups=mesh['row'=8,'col'=16] {'row','col'}, dimensions={0} | all-to-all | bytes 524288 | tf_op jit(solution)/shard_map/all_to_all | solution.py:15
  36.6 12.8 %all_to_all.32 = bf16[8,64,512]{2,1,0:T(8,128)(2,1)S(1)} all-to-all(bf16[8,64,512]{2,1,0:T(8,128)(2,1)S(1)} %broadcast_in_dim.16), channel_id=1, replica_groups=mesh['row'=8,'col'=16] {'row'}, dimensions={0} | all-to-all | bytes 1048576 | tf_op jit(solution)/shard_map/all_to_all | solution.py:35
  56.9 5.6 %convolution_convert_fusion = bf16[32,131072]{1,0:T(8,128)(2,1)} fusion(bf16[2,131072]{1,0:T(2,128)(2,1)S(1)} %reshape_reshape.6, s32[32]{0:T(128)S(1)} %compare_select_fusion.6), kind=kOutput, calls=%fused_computation.8 | convolution fusion | flops 20971584 | bytes 8913024 | tf_op jit(solution)/shard_map/dot_general | solution.py:152
  62.5 9.4 %reshape.631 = bf16[16,2,131072]{2,1,0:T(2,128)(2,1)} reshape(bf16[32,131072]{1,0:T(8,128)(2,1)} %convolution_convert_fusion) | data formatting | bytes 16777216 | tf_op jit(solution)/shard_map/reshape | solution.py:158
  71.8 13.9 %all-to-all-done.4 = bf16[16,2,64,512]{3,2,1,0:T(8,128)(2,1)S(1)} async-done(((bf16[16,2,64,512]{3,2,1,0:T(8,128)(2,1)}), bf16[16,2,64,512]{3,2,1,0:T(8,128)(2,1)S(1)}, u32[]{:S(2)}, u32[]{:S(2)}) %all-to-all-start.4) | async-done | bytes 2097184 | tf_op jit(solution)/shard_map/all_to_all | solution.py:35
  97.2 8.9 %slice_reduce_fusion.19 = (f32[8192]{0:T(1024)S(1)}, f32[8192]{0:T(1024)S(1)}, f32[8192,1]{1,0:T(8,128)}, f32[8192,1]{1,0:T(8,128)}) fusion(f32[8192,8]{1,0:T(8,128)} %bitcast.99), kind=kLoop, calls=%fused_computation.112 | loop fusion | bytes 196608 | tf_op jit(solution)/shard_map/slice | solution.py:21
  106.1 11.8 %gather_fusion.4 = f32[2048]{0:T(1024)S(1)} fusion(f32[8192]{0:T(1024)S(1)} %get-tuple-element.6, s32[2048]{0:T(1024)S(1)} %fusion.27), kind=kCustom, calls=%fused_computation.3.clone | custom fusion | bytes 24576 | tf_op jit(solution)/shard_map/jit(_take)/gather | solution.py:180
  117.8 11.8 %gather_fusion = f32[2048]{0:T(1024)S(1)} fusion(f32[8192]{0:T(1024)S(1)} %get-tuple-element.6, s32[2048]{0:T(1024)S(1)} %fusion.26), kind=kCustom, calls=%fused_computation.clone | custom fusion | bytes 24576 | tf_op jit(solution)/shard_map/jit(_take)/gather | solution.py:180
  129.6 11.8 %gather_fusion.6 = f32[2048]{0:T(1024)S(1)} fusion(f32[8192]{0:T(1024)S(1)} %get-tuple-element.8, s32[2048]{0:T(1024)S(1)} %fusion.27), kind=kCustom, calls=%fused_computation.4.clone | custom fusion | bytes 24576 | tf_op jit(solution)/shard_map/jit(_take)/gather | solution.py:182
  141.4 11.8 %gather_fusion.2 = f32[2048]{0:T(1024)S(1)} fusion(f32[8192]{0:T(1024)S(1)} %get-tuple-element.8, s32[2048]{0:T(1024)S(1)} %fusion.26), kind=kCustom, calls=%fused_computation.2.clone | custom fusion | bytes 24576 | tf_op jit(solution)/shard_map/jit(_take)/gather | solution.py:182
  153.2 10.6 %slice_bitcast_fusion.3 = (f32[3,8192]{0,1:T(8,128)}, f32[3,8192]{0,1:T(8,128)}, f32[8192,3]{1,0:T(8,128)}, f32[8192,3]{1,0:T(8,128)}) fusion(f32[8192,8]{1,0:T(8,128)} %bitcast.100), kind=kLoop, calls=%fused_computation.111 | loop fusion | bytes 589824 | tf_op jit(solution)/shard_map/transpose | solution.py:22
  163.8 7.6 %gather_fusion.5 = f32[2048,3]{1,0:T(8,128)S(1)} fusion(f32[3,8192]{0,1:T(8,128)} %get-tuple-element.33, s32[2048]{0:T(1024)S(1)} %fusion.27), kind=kCustom, calls=%fused_computation.6.clone | custom fusion | bytes 57344 | tf_op jit(solution)/shard_map/jit(_take)/gather | solution.py:179
  171.4 7.6 %gather_fusion.1 = f32[2048,3]{1,0:T(8,128)S(1)} fusion(f32[3,8192]{0,1:T(8,128)} %get-tuple-element.33, s32[2048]{0:T(1024)S(1)} %fusion.26), kind=kCustom, calls=%fused_computation.1.clone | custom fusion | bytes 57344 | tf_op jit(solution)/shard_map/jit(_take)/gather | solution.py:179
  179.1 9.7 %gather_fusion.3 = f32[2048,3]{1,0:T(8,128)} fusion(f32[3,8192]{0,1:T(8,128)} %get-tuple-element.34, s32[2048]{0:T(1024)S(1)} %fusion.26), kind=kCustom, calls=%fused_computation.5.clone | custom fusion | bytes 57344 | tf_op jit(solution)/shard_map/jit(_take)/gather | solution.py:181
  188.8 9.9 %gather_fusion.7 = f32[2048,3]{1,0:T(8,128)} fusion(f32[3,8192]{0,1:T(8,128)} %get-tuple-element.34, s32[2048]{0:T(1024)S(1)} %fusion.27), kind=kCustom, calls=%fused_computation.7.clone | custom fusion | bytes 57344 | tf_op jit(solution)/shard_map/jit(_take)/gather | solution.py:181
  212.4 33.1 %fusion.5 = (f32[1024,4,256]{0,2,1:T(8,128)}, f32[1024,4,256]{0,2,1:T(8,128)}) fusion(f32[1024]{0:T(1024)S(1)} %bitcast.118, f32[1024]{0:T(1024)S(1)} %bitcast.121, f32[1024]{0:T(1024)S(1)} %bitcast.115, f32[4,256]{1,0:T(4,128)S(1)} %mul.505, f32[4,256]{1,0:T(4,128)S(1)} %mul.502, f32[4,256]{1,0:T(4,128)S(1)} %mul.499, f32[4,256]{1,0:T(4,128)S(1)} %add.256, ...), kind=kLoop, calls=%fused_computation.25 | loop fusion | flops 37748736 | bytes 8445952 | tf_op jit(solution)/shard_map/convert_element_type | solution.py:80
  247.1 8.6 %reshape.632 = bf16[32,131072]{1,0:T(8,128)(2,1)} reshape(bf16[16,2,131072]{2,1,0:T(2,128)(2,1)} %all-to-all-done.2) | data formatting | bytes 16777216 | tf_op jit(solution)/shard_map/reshape | solution.py:163
  272.1 33.9 %fusion.2 = f32[1024,512]{0,1:T(8,128)S(1)} fusion(f32[1024,4,256]{0,2,1:T(8,128)S(1)} %copy-done, bf16[4,512,512]{1,2,0:T(8,128)(2,1)S(1)} %bitcast.107, f32[4,512]{1,0:T(4,128)S(1)} %mul.529, f32[4,512]{1,0:T(4,128)S(1)} %mul.526, f32[4,512]{1,0:T(4,128)S(1)} %mul.523, f32[4,512]{1,0:T(4,128)S(1)} %add.263, f32[4,512]{1,0:T(4,128)S(1)} %sub.262, ...), kind=kOutput, calls=%fused_computation.16 | convolution fusion | flops 2186805248 | bytes 8466432 | tf_op jit(solution)/shard_map/gax,axy->gay/dot_general | solution.py:76
  306.1 33.6 %fusion = f32[1024,512]{0,1:T(8,128)S(1)} fusion(f32[1024,4,256]{0,2,1:T(8,128)S(1)} %copy-done.1, bf16[4,512,512]{1,2,0:T(8,128)(2,1)S(1)} %bitcast.106, f32[4,512]{1,0:T(4,128)S(1)} %mul.484, f32[4,512]{1,0:T(4,128)S(1)} %mul.481, f32[4,512]{1,0:T(4,128)S(1)} %mul.478, f32[4,512]{1,0:T(4,128)S(1)} %add.248, f32[4,512]{1,0:T(4,128)S(1)} %sub.235, ...), kind=kOutput, calls=%fused_computation.14 | convolution fusion | flops 2186805248 | bytes 8466432 | tf_op jit(solution)/shard_map/gax,axy->gay/dot_general | solution.py:76
  341.7 33.7 %convolution_convert_fusion.3 = bf16[4,512,512]{1,2,0:T(8,128)(2,1)S(1)} fusion(bf16[1024,4,512]{0,2,1:T(8,128)(2,1)S(1)} %fusion.1, f32[4,512]{1,0:T(4,128)S(1)} %mul.484, f32[4,512]{1,0:T(4,128)S(1)} %mul.481, f32[4,512]{1,0:T(4,128)S(1)} %mul.478, f32[4,512]{1,0:T(4,128)S(1)} %add.248, f32[4,512]{1,0:T(4,128)S(1)} %sub.235, f32[1024]{0:T(1024)S(1)} %bitcast.126, ...), kind=kOutput, calls=%fused_computation.38 | convolution fusion | flops 2184183808 | bytes 6369280 | tf_op jit(solution)/shard_map/gax,gay->axy/dot_general | solution.py:89
  378.5 42.9 %convolution_convert_fusion.2 = bf16[4,512,512]{1,2,0:T(8,128)(2,1)S(1)} fusion(bf16[1024,4,512]{0,2,1:T(8,128)(2,1)S(1)} %fusion.3, f32[4,512]{1,0:T(4,128)S(1)} %mul.529, f32[4,512]{1,0:T(4,128)S(1)} %mul.526, f32[4,512]{1,0:T(4,128)S(1)} %mul.523, f32[4,512]{1,0:T(4,128)S(1)} %add.263, f32[4,512]{1,0:T(4,128)S(1)} %sub.262, f32[1024]{0:T(1024)S(1)} %bitcast.120, ...), kind=kOutput, calls=%fused_computation.37 | convolution fusion | flops 2184183808 | bytes 6369280 | tf_op jit(solution)/shard_map/gax,gay->axy/dot_general | solution.py:89
  423.2 32.2 %all_to_all.33 = bf16[16,64,2,512]{3,1,2,0:T(8,128)(2,1)S(1)} all-to-all(bf16[16,64,2,512]{3,1,2,0:T(8,128)(2,1)S(1)} %copy.31), channel_id=1, replica_groups=mesh['row'=8,'col'=16] {'col'}, dimensions={0} | all-to-all | bytes 4194304 | tf_op jit(solution)/shard_map/all_to_all | solution.py:52
  (111 shorter events, 63.4 us)
Async XLA Ops:
  3.2 14.7 %all-to-all-start = ((s32[16,1,2]{2,1,0:T(1,128)}), s32[16,1,2]{2,1,0:T(1,128)S(1)}, u32[]{:S(2)}, u32[]{:S(2)}) async-start(s32[16,1,2]{2,1,0:T(1,128)} %bitcast), calls=%async_computation | async-start | bytes 16384 | tf_op jit(solution)/shard_map/all_to_all | solution.py:131
  51.8 33.9 %all-to-all-start.4 = ((bf16[16,2,64,512]{3,2,1,0:T(8,128)(2,1)}), bf16[16,2,64,512]{3,2,1,0:T(8,128)(2,1)S(1)}, u32[]{:S(2)}, u32[]{:S(2)}) async-start(bf16[16,2,64,512]{3,2,1,0:T(8,128)(2,1)} %broadcast_in_dim.17), calls=%async_computation.4 | async-start | bytes 4194304 | tf_op jit(solution)/shard_map/all_to_all | solution.py:35
  71.8 20.6 %copy-start.7 = (f32[2,1024]{1,0:T(2,128)S(1)}, f32[2,1024]{1,0:T(2,128)}, u32[]{:S(2)}) copy-start(f32[2,1024]{1,0:T(2,128)} %param.21) | copy-start | bytes 24580
  71.8 20.6 %copy-start.8 = (f32[2,1024]{1,0:T(2,128)S(1)}, f32[2,1024]{1,0:T(2,128)}, u32[]{:S(2)}) copy-start(f32[2,1024]{1,0:T(2,128)} %param.22) | copy-start | bytes 24580
  71.8 20.7 %copy-start.6 = (f32[2,3,1024]{2,0,1:T(2,128)S(1)}, f32[2,3,1024]{2,0,1:T(2,128)}, u32[]{:S(2)}) copy-start(f32[2,3,1024]{2,0,1:T(2,128)} %param.20) | copy-start | bytes 73732
  85.8 1.4 copy-start.3
  87.1 159.9 %all-to-all-start.2 = ((bf16[16,2,131072]{2,1,0:T(2,128)(2,1)}), bf16[16,2,131072]{2,1,0:T(2,128)(2,1)}, u32[]{:S(2)}, u32[]{:S(2)}) async-start(bf16[16,2,131072]{2,1,0:T(2,128)(2,1)} %reshape.631), calls=%async_computation.2 | async-start | bytes 16777216 | tf_op jit(solution)/shard_map/all_to_all | solution.py:160
  212.3 33.1 %copy-start.4 = (bf16[16,2,64,512]{3,2,1,0:T(8,128)(2,1)S(1)}, bf16[16,2,64,512]{3,2,1,0:T(8,128)(2,1)}, u32[]{:S(2)}) copy-start(bf16[16,2,64,512]{3,2,1,0:T(8,128)(2,1)} %copy-done.3) | copy-start | bytes 6291460
  266.8 3.1 copy-start.2
  266.8 3.1 copy-start.5
  269.9 2.2 copy-start
  272.1 34.0 %copy-start.1 = (f32[1024,4,256]{0,2,1:T(8,128)S(1)}, f32[1024,4,256]{0,2,1:T(8,128)}, u32[]{:S(2)}) copy-start(f32[1024,4,256]{0,2,1:T(8,128)} %get-tuple-element.40) | copy-start | bytes 12582916
